TPU v7x, 256 devices: a 4x2x16 block of a 4x16x16 slice. The times are simulated.
256 devices in a mesh: rep: 2 (over y), gx: 128 (over x, z, core).
Axes of the slice: x: 4, y: 2, z: 16, core: 2. Of those that a mesh axis runs over, the one named last changes fastest.
The devices are a block of a 4x16x16 slice.
Arguments:
- positions: float32 [3, 262144], P(None, ('rep', 'gx')), parts along dimension 1, may hold values from 0 to 8, as said below
- field: float32 [3, 262144], P(None, ('rep', 'gx')), parts along dimension 1, may hold values from -45 to 45
- inv_polar: float32 [262144], P(('rep', 'gx')), parts along dimension 0, may hold values from 2 to 8
- x_spline: float32 [2, 5, 262144], P(None, None, ('rep', 'gx')), parts along dimension 2, may hold values from -1 to 1, as said below
- yz_spline: float32 [4, 262144, 128], P(None, ('rep', 'gx')), parts along dimension 1, may hold values from -1 to 1, as said below
- tile_list: int32 [2048, 7], P(('rep', 'gx')), parts along dimension 0, may hold values from 0 to 13, as said below
- tile_count: int32 [2048], P(('rep', 'gx')), parts along dimension 0, may hold values from 1 to 7, as said below
Outputs:
- dipoles: float32 [3, 262144], P(None, ('rep', 'gx')), parts along dimension 1
- residual: float32 [3, 262144], P(None, ('rep', 'gx')), parts along dimension 1
There are 2 independent parts, one for each index of `rep`. A program takes and returns all parts, laid end to end along the dimension named above; each array names one. Nothing has to cross between parts.
Inputs may be any that keep to these rules, and one draw needn't show every extreme that they name: `positions`: the first coordinate of an atom of block b of its slab lies in [b, b + 1); the other two lie in [0, 2). x_spline[0, k, i] and x_spline[1, k, i] are the cardinal B-spline of order 5 and its derivative at u_i + 4 - k for some u_i in [0, 1). `yz_spline`: rows 0 and 1 hold, for each atom, the cardinal B-spline of order 5 and its derivative at u + 4 - k placed at grid line (t + k) mod 128 for k < 5, for some start t and some u in [0, 1), and zero elsewhere; rows 2 and 3 likewise with their own start and offset. `tile_list`: row g = s * 8 + b lists in rising order the extended blocks b + 3 + e, -3 <= e <= 3, for which global blocks g and g + e (modulo 1024) are neighbours; being neighbours is symmetric and always holds for e = 0; entries from tile_count[g] on equal b + 3. `tile_count`: global block 0 has all 7 neighbours.
All inputs are finite; a program needn't handle non-finite values.
Results may differ from a plain program's by a relative error of at most 0.0003.
Values sent between devices are 32-bit elements; how exact they have to be, the bound alone decides.
A program may use at most 64 MiB of HBM per device.

v0:
```python
import jax
import jax.numpy as jnp
from jax import lax
from jax.sharding import Mesh
from jax.sharding import PartitionSpec as P

GRID = 128
ORDER = 5
TILE = 128
HALO_BLK = 3
ITERS = 3
GX = ("gx_0", "gx_1", "gx_2")
REP_GX = ("rep", "gx_0", "gx_1", "gx_2")
PAIR_C = 0.025
RECIP_C = 8192.0
DAMP = 0.0008
EXACT = lax.Precision.HIGHEST


def from_behind(x, axis, by):
    devices = lax.axis_size(axis)
    return lax.ppermute(x, axis, [(i, (i + by) % devices) for i in range(devices)])


def extended(x, sides, width):
    for axis, dim in sides:
        devices, length = (lax.axis_size(axis), x.shape[dim])
        up = [(i, (i + 1) % devices) for i in range(devices)]
        down = [(j, i) for i, j in up]
        last = lax.slice_in_dim(x, length - width, length, axis=dim)
        first = lax.slice_in_dim(x, 0, width, axis=dim)
        before = lax.ppermute(last, axis, up)
        after = lax.ppermute(first, axis, down)
        x = jnp.concatenate([before, x, after], axis=dim)
    return x


def split_up(x, dim, devices):
    before, after = (x.shape[:dim], x.shape[dim + 1 :])
    return jnp.moveaxis(x.reshape(*before, devices, -1, *after), dim, 0)


def in_order(tiles, dim):
    dims = list(tiles.shape[1:])
    dims[dim] *= tiles.shape[0]
    return jnp.moveaxis(tiles, 0, dim).reshape(dims)


def turned_blocks(tiles, axes, sequence):
    dims = [lax.axis_size(a) for a in axes]
    tiles = tiles.reshape(*dims, *tiles.shape[1:])
    for k in sequence:
        tiles = lax.all_to_all(tiles, axes[k], split_axis=k, concat_axis=k, tiled=True)
    return tiles.reshape(-1, *tiles.shape[len(axes) :])


def exchange_by_chip(x, groups, sequence, split_dim, concat_dim):
    devices = lax.axis_size(groups[0]) * lax.axis_size(groups[1])
    tiles = split_up(x, split_dim, devices)
    return in_order(turned_blocks(tiles, groups, sequence), concat_dim)


def over_axes(x, axes):
    for axis in axes:
        x = lax.psum(x, axis)
    return x


def pair_field(home_pos, ext_pos, ext_vec, tile_rows, live_counts):
    slab_blocks = home_pos.shape[1] // TILE
    ext_blocks = ext_pos.shape[1] // TILE
    home_blocks = home_pos.reshape(3, slab_blocks, TILE).transpose(1, 0, 2)
    pos_blocks = ext_pos.reshape(3, ext_blocks, TILE)
    vec_blocks = ext_vec.reshape(3, ext_blocks, TILE)
    slot_index = jnp.arange(tile_rows.shape[1], dtype=jnp.int32)
    self_pair = jnp.eye(TILE, dtype=bool)

    def one_block(carried, scan_item):
        home_block, tile_row, live_count, block_index = scan_item
        near_pos = jnp.take(pos_blocks, tile_row, axis=1)
        near_vec = jnp.take(vec_blocks, tile_row, axis=1)
        offsets = home_block[:, None, :, None] - near_pos[:, :, None, :]
        distance_sq = jnp.sum(offsets * offsets, axis=0) + 1.0
        inverse = lax.rsqrt(distance_sq)
        third_power = inverse * inverse * inverse
        fifth_power = third_power * inverse * inverse
        same_block = (tile_row == block_index + HALO_BLK)[:, None, None]
        live_mask = (slot_index < live_count)[:, None, None] & ~(same_block & self_pair[None])
        third_power = jnp.where(live_mask, third_power, 0.0)
        fifth_power = jnp.where(live_mask, fifth_power, 0.0)
        projection = jnp.sum(offsets * near_vec[:, :, None, :], axis=0)
        field_sum = jnp.sum(
            third_power[None] * near_vec[:, :, None, :]
            - 3.0 * (fifth_power * projection)[None] * offsets,
            axis=(1, 3),
        )
        return (carried, PAIR_C * field_sum)

    block_ids = jnp.arange(slab_blocks, dtype=jnp.int32)
    unused_carry, blocks_out = lax.scan(
        one_block, jnp.zeros((), jnp.float32), (home_blocks, tile_rows, live_counts, block_ids)
    )
    return blocks_out.transpose(1, 0, 2).reshape(3, slab_blocks * TILE)


def slab_weights(local_plane, x_spline, planes):
    spline_steps = jnp.arange(ORDER, dtype=jnp.int32)
    plane_index = jnp.arange(planes, dtype=jnp.int32)
    matches = local_plane[None, :, None] + spline_steps[:, None, None] == plane_index[None, None, :]
    spline_value = jnp.sum(jnp.where(matches, x_spline[0][:, :, None], 0.0), axis=0)
    spline_slope = jnp.sum(jnp.where(matches, x_spline[1][:, :, None], 0.0), axis=0)
    return (spline_value, spline_slope)


def spread_dipoles(vector, spline_value, spline_slope, yz_spline):
    atoms_here = spline_value.shape[0]
    planes = spline_value.shape[1]
    grid_lines = yz_spline.shape[2]
    lead_terms = (vector[0][:, None] * spline_slope)[:, :, None] * yz_spline[0][:, None, :]
    lead_terms = (
        lead_terms + (vector[1][:, None] * spline_value)[:, :, None] * yz_spline[1][:, None, :]
    )
    tail_terms = (vector[2][:, None] * spline_value)[:, :, None] * yz_spline[0][:, None, :]
    contract = (((0,), (0,)), ((), ()))
    charge = lax.dot_general(
        lead_terms.reshape(atoms_here, planes * grid_lines), yz_spline[2], contract, precision=EXACT
    )
    charge = charge + lax.dot_general(
        tail_terms.reshape(atoms_here, planes * grid_lines), yz_spline[3], contract, precision=EXACT
    )
    return charge.reshape(planes, grid_lines, grid_lines)


def gather_field(potential, spline_value, spline_slope, yz_spline):
    planes = potential.shape[0]
    grid_lines = potential.shape[1]
    atoms_here = spline_value.shape[0]
    flat_grid = potential.reshape(planes * grid_lines, grid_lines)
    contract = (((1,), (1,)), ((), ()))
    plain_sum = lax.dot_general(yz_spline[2], flat_grid, contract, precision=EXACT).reshape(
        atoms_here, planes, grid_lines
    )
    tilted_sum = lax.dot_general(yz_spline[3], flat_grid, contract, precision=EXACT).reshape(
        atoms_here, planes, grid_lines
    )
    first_comp = jnp.sum(
        spline_slope[:, :, None] * yz_spline[0][:, None, :] * plain_sum, axis=(1, 2)
    )
    second_comp = jnp.sum(
        spline_value[:, :, None] * yz_spline[1][:, None, :] * plain_sum, axis=(1, 2)
    )
    third_comp = jnp.sum(
        spline_value[:, :, None] * yz_spline[0][:, None, :] * tilted_sum, axis=(1, 2)
    )
    return jnp.stack([first_comp, second_comp, third_comp])


def mode_of(freq, size):
    half_size = size // 2
    mode_num = jnp.where(freq <= half_size, freq, freq - half_size)
    weight = jnp.where((freq == 0) | (freq == half_size), 1.0 / size, 2.0 / size)
    return (mode_num.astype(jnp.float32), weight.astype(jnp.float32))


def basis_rows(size, points):
    freq = jnp.arange(size, dtype=jnp.int32)
    half_size = size // 2
    mode_num = jnp.where(freq <= half_size, freq, freq - half_size)
    phase = mode_num[:, None] * points[None, :] % size
    angle = phase.astype(jnp.float32) * (2.0 * jnp.pi / size)
    return jnp.where((freq <= half_size)[:, None], jnp.cos(angle), jnp.sin(angle))


def kernel_block(x_modes, x_weights, y_modes, y_weights, z_modes, z_weights):
    mode_sq = (
        x_modes[:, None, None] * x_modes[:, None, None]
        + y_modes[None, :, None] * y_modes[None, :, None]
        + z_modes[None, None, :] * z_modes[None, None, :]
    )
    safe_sq = jnp.where(mode_sq > 0, mode_sq, 1.0)
    green = jnp.where(mode_sq > 0, RECIP_C * jnp.exp(-DAMP * safe_sq) / safe_sq, 0.0)
    return green * x_weights[:, None, None] * y_weights[None, :, None] * z_weights[None, None, :]


def forward_lines(charge, fourier_rows):
    along_z = jnp.einsum("pyz,kz->pyk", charge, fourier_rows, precision=EXACT)
    return jnp.einsum("jy,pyk->pjk", fourier_rows, along_z, precision=EXACT)


def inverse_lines(spectrum, fourier_rows):
    along_z = jnp.einsum("pjk,kz->pjz", spectrum, fourier_rows, precision=EXACT)
    return jnp.einsum("jy,pjz->pyz", fourier_rows, along_z, precision=EXACT)


def from_above(piece, distance):
    return from_behind(piece, GX, -distance)


def from_below(piece, distance):
    return from_behind(piece, GX, distance)


def per_device(positions, field, inv_polar, x_spline, yz_spline, tile_list, tile_count):
    rank_count = lax.axis_size(GX)
    rank_index = lax.axis_index(GX)
    atoms_here = positions.shape[1]
    planes = GRID // rank_count
    extent = planes + 4
    halo_atoms = HALO_BLK * TILE
    slab_blocks = atoms_here // TILE
    local_plane = jnp.arange(atoms_here, dtype=jnp.int32) * planes // atoms_here
    spline_value, spline_slope = slab_weights(local_plane, x_spline, extent)
    ext_pos = extended(positions, ((GX, 1),), halo_atoms)
    shift_x = jnp.concatenate(
        [
            jnp.full((halo_atoms,), -1.0 * slab_blocks, jnp.float32),
            jnp.zeros((atoms_here,), jnp.float32),
            jnp.full((halo_atoms,), 1.0 * slab_blocks, jnp.float32),
        ]
    )
    ext_pos = ext_pos.at[0].add(shift_x)
    fourier_rows = basis_rows(GRID, jnp.arange(GRID, dtype=jnp.int32))
    ky_count = GRID // rank_count
    all_freq = jnp.arange(GRID, dtype=jnp.int32)
    ky_freq = rank_index * ky_count + jnp.arange(ky_count, dtype=jnp.int32)
    full_modes, full_weights = mode_of(all_freq, GRID)
    ky_modes, ky_weights = mode_of(ky_freq, GRID)
    kernel = kernel_block(full_modes, full_weights, ky_modes, ky_weights, full_modes, full_weights)
    kernel = kernel.reshape(GRID, ky_count * GRID)

    def reciprocal(charge):
        rim_planes = min(2, planes)
        hop_count = (planes + 1) // planes
        owned_planes = charge[2 : 2 + planes]
        for distance in range(1, hop_count + 1):
            lower_piece = charge[2 - distance * rim_planes : 2 - (distance - 1) * rim_planes]
            owned_planes = owned_planes.at[planes - rim_planes :].add(
                from_above(lower_piece, distance)
            )
            upper_piece = charge[
                planes + 2 + (distance - 1) * rim_planes : planes + 2 + distance * rim_planes
            ]
            owned_planes = owned_planes.at[:rim_planes].add(from_below(upper_piece, distance))
        spectrum = forward_lines(owned_planes, fourier_rows)
        pencils = exchange_by_chip(spectrum, (("gx_0", "gx_1"), "gx_2"), (1, 0), 1, 0)
        flat_pencils = pencils.reshape(GRID, ky_count * GRID)
        spectral_lines = jnp.dot(fourier_rows, flat_pencils, precision=EXACT) * kernel
        returned_lines = lax.dot_general(
            fourier_rows, spectral_lines, (((0,), (0,)), ((), ())), precision=EXACT
        )
        returned = exchange_by_chip(
            returned_lines.reshape(GRID, ky_count, GRID), (("gx_0", "gx_1"), "gx_2"), (1, 0), 0, 1
        )
        own_potential = inverse_lines(returned, fourier_rows)
        below_parts = [from_below(own_potential, distance) for distance in range(hop_count, 0, -1)]
        above_parts = [from_above(own_potential, distance) for distance in range(1, hop_count + 1)]
        return jnp.concatenate(below_parts + [own_potential] + above_parts, axis=0)

    def apply(vector):
        ext_vec = extended(vector, ((GX, 1),), halo_atoms)
        near_field = pair_field(positions, ext_pos, ext_vec, tile_list, tile_count)
        charge = spread_dipoles(vector, spline_value, spline_slope, yz_spline)
        far_field = gather_field(reciprocal(charge), spline_value, spline_slope, yz_spline)
        return inv_polar[None, :] * vector + far_field - near_field

    def paired(residual, precond, applied):
        return (
            over_axes(jnp.sum(residual * precond), GX),
            over_axes(jnp.sum(applied * precond), GX),
        )

    dipoles = jnp.zeros_like(field)
    residual = field
    precond = field / inv_polar[None, :]
    applied = apply(precond)
    rz_now, curvature = paired(residual, precond, applied)
    step_size = rz_now / curvature
    direction = precond
    applied_dir = applied
    for sweep_index in range(ITERS):
        dipoles = dipoles + step_size * direction
        residual = residual - step_size * applied_dir
        if sweep_index + 1 < ITERS:
            precond = residual / inv_polar[None, :]
            applied = apply(precond)
            rz_next, curvature = paired(residual, precond, applied)
            beta_ratio = rz_next / rz_now
            step_size = rz_next / (curvature - beta_ratio * rz_next / step_size)
            direction = precond + beta_ratio * direction
            applied_dir = applied + beta_ratio * applied_dir
            rz_now = rz_next
    return (dipoles, residual)


def solution(mesh):
    torus = Mesh(mesh.devices.reshape(mesh.shape["rep"], 4, 16, 2), ("rep", "gx_0", "gx_1", "gx_2"))
    in_specs = (
        P(None, REP_GX),
        P(None, REP_GX),
        P(REP_GX),
        P(None, None, REP_GX),
        P(None, REP_GX, None),
        P(REP_GX, None),
        P(REP_GX),
    )
    out_specs = (P(None, REP_GX), P(None, REP_GX))
    return jax.shard_map(
        per_device, mesh=torus, in_specs=in_specs, out_specs=out_specs, check_vma=False
    )
```

profile of v0, /device:TPU:33, one launch (start us, length us, event | category | flops | bytes accessed | tf_op | source)
XLA Modules:
  0.0 596.3 jit_solution(14503698682587773255)
XLA Ops:
  15.9 20.4 %collective-permute-start = (f32[1,128,128]{2,1,0:T(8,128)}, f32[1,128,128]{2,1,0:T(8,128)}, u32[]{:S(2)}, u32[]{:S(2)}) collective-permute-start(f32[1,128,128]{2,1,0:T(8,128)} %get-tuple-element.678), channel_id=1, source_target_pairs={{0,127},{1,0},{2,1},{3,2},{4,3},{5,4},{6,5},{7,6},{8,7},{9,8},{10,... | collective-permute-start | bytes 196616 | tf_op jit(solution)/shard_map/ppermute | solution.py:22
  36.4 10.2 %collective-permute-start.2 = (f32[1,128,128]{2,1,0:T(8,128)}, f32[1,128,128]{2,1,0:T(8,128)}, u32[]{:S(2)}, u32[]{:S(2)}) collective-permute-start(f32[1,128,128]{2,1,0:T(8,128)} %get-tuple-element.680), channel_id=1, source_target_pairs={{0,126},{1,127},{2,0},{3,1},{4,2},{5,3},{6,4},{7,5},{8,6},{9,7},{1... | collective-permute-start | bytes 196616 | tf_op jit(solution)/shard_map/ppermute | solution.py:22
  59.0 8.5 %all_to_all.60 = f32[64,2,1,1,128]{4,0,3,2,1:T(8,128)S(1)} all-to-all(f32[64,2,1,1,128]{4,0,3,2,1:T(8,128)S(1)} %copy.68), channel_id=1, replica_groups=mesh['rep'=2,'gx_0'=4,'gx_1'=16,'gx_2'=2] {'gx_2'}, dimensions={1} | all-to-all | bytes 131072 | tf_op jit(solution)/shard_map/all_to_all | solution.py:53
  68.2 6.5 %all-to-all-start.1 = ((f32[64,2,1,1,128]{4,1,3,2,0:T(2,128)}), f32[64,2,1,1,128]{4,1,3,2,0:T(2,128)S(1)}, u32[]{:S(2)}, u32[]{:S(2)}) async-start(f32[64,2,1,1,128]{4,1,3,2,0:T(2,128)} %copy.69), calls=%async_computation.1 | async-start | bytes 131072 | tf_op jit(solution)/shard_map/all_to_all | solution.py:53
  76.1 10.7 %all-to-all-done.1 = f32[64,2,1,1,128]{4,1,3,2,0:T(2,128)S(1)} async-done(((f32[64,2,1,1,128]{4,1,3,2,0:T(2,128)}), f32[64,2,1,1,128]{4,1,3,2,0:T(2,128)S(1)}, u32[]{:S(2)}, u32[]{:S(2)}) %all-to-all-start.1) | async-done | bytes 65568 | tf_op jit(solution)/shard_map/all_to_all | solution.py:53
  95.5 6.5 %all-to-all-start.3 = ((f32[64,2,1,1,128]{4,1,3,2,0:T(2,128)}), f32[64,2,1,1,128]{4,1,3,2,0:T(2,128)S(1)}, u32[]{:S(2)}, u32[]{:S(2)}) async-start(f32[64,2,1,1,128]{4,1,3,2,0:T(2,128)} %copy.71), calls=%async_computation.3 | async-start | bytes 131072 | tf_op jit(solution)/shard_map/all_to_all | solution.py:53
  103.5 10.6 %all-to-all-done.3 = f32[64,2,1,1,128]{4,1,3,2,0:T(2,128)S(1)} async-done(((f32[64,2,1,1,128]{4,1,3,2,0:T(2,128)}), f32[64,2,1,1,128]{4,1,3,2,0:T(2,128)S(1)}, u32[]{:S(2)}, u32[]{:S(2)}) %all-to-all-start.3) | async-done | bytes 65568 | tf_op jit(solution)/shard_map/all_to_all | solution.py:53
  115.8 43.6 %while.58 = (s32[]{:T(128)}, f32[8,3,128]{2,1,0:T(4,128)S(1)}, s32[8]{0:T(128)S(1)}, s32[8,7]{1,0:T(8,128)}, s32[8]{0:T(128)S(1)}, /*index=5*/f32[8,3,128]{2,1,0...) while((s32[]{:T(128)}, f32[8,3,128]{2,1,0:T(4,128)S(1)}, ...), condition=%wide.region_13.15_spmd.clone, body=%wide.region_9.14_spmd.clone.sunk | while | flops 4610363 | bytes 3891027 | solution.py:100
  176.7 6.7 %all-reduce.5 = (f32[]{:T(128)}, f32[]{:T(128)}) all-reduce(f32[]{:T(128)} %get-tuple-element.562, f32[]{:T(128)} %get-tuple-element.561), channel_id=1, replica_groups=mesh['rep'=2,'gx_0'=4,'gx_1'=16,'gx_2'=2] {'gx_0'}, use_global_device_ids=true, to_apply=%region_1.2 | all-reduce | flops 2 | bytes 16 | tf_op jit(solution)/shard_map/psum | solution.py:65
  183.3 26.5 %all-reduce.2 = (f32[]{:T(128)}, f32[]{:T(128)}) all-reduce(f32[]{:T(128)} %get-tuple-element.621, f32[]{:T(128)} %get-tuple-element.622), channel_id=1, replica_groups=mesh['rep'=2,'gx_0'=4,'gx_1'=16,'gx_2'=2] {'gx_1'}, use_global_device_ids=true, to_apply=%region_2.3 | all-reduce | flops 2 | bytes 16 | tf_op jit(solution)/shard_map/psum | solution.py:65
  209.9 13.9 %all-reduce.8 = (f32[]{:T(128)}, f32[]{:T(128)}) all-reduce(f32[]{:T(128)} %get-tuple-element.615, f32[]{:T(128)} %get-tuple-element.616), channel_id=1, replica_groups=mesh['rep'=2,'gx_0'=4,'gx_1'=16,'gx_2'=2] {'gx_2'}, use_global_device_ids=true, to_apply=%region_3.4 | all-reduce | flops 2 | bytes 16 | tf_op jit(solution)/shard_map/psum | solution.py:65
  248.5 17.8 %all_to_all.63 = f32[64,2,1,1,128]{4,1,3,2,0:T(2,128)S(1)} all-to-all(f32[64,2,1,1,128]{4,1,3,2,0:T(2,128)S(1)} %copy.75), channel_id=1, replica_groups=mesh['rep'=2,'gx_0'=4,'gx_1'=16,'gx_2'=2] {'gx_0','gx_1'}, dimensions={0} | all-to-all | bytes 131072 | tf_op jit(solution)/shard_map/all_to_all | solution.py:53
  273.6 6.5 %all-to-all-start.7 = ((f32[64,2,1,1,128]{4,1,3,2,0:T(2,128)}), f32[64,2,1,1,128]{4,1,3,2,0:T(2,128)S(1)}, u32[]{:S(2)}, u32[]{:S(2)}) async-start(f32[64,2,1,1,128]{4,1,3,2,0:T(2,128)} %copy.77), calls=%async_computation.7 | async-start | bytes 131072 | tf_op jit(solution)/shard_map/all_to_all | solution.py:53
  284.3 7.9 %all-to-all-done.7 = f32[64,2,1,1,128]{4,1,3,2,0:T(2,128)S(1)} async-done(((f32[64,2,1,1,128]{4,1,3,2,0:T(2,128)}), f32[64,2,1,1,128]{4,1,3,2,0:T(2,128)S(1)}, u32[]{:S(2)}, u32[]{:S(2)}) %all-to-all-start.7) | async-done | bytes 65568 | tf_op jit(solution)/shard_map/all_to_all | solution.py:53
  294.4 48.8 %while.59 = (s32[]{:T(128)}, f32[8,3,128]{2,1,0:T(4,128)S(1)}, s32[8]{0:T(128)S(1)}, s32[8,7]{1,0:T(8,128)}, s32[8]{0:T(128)}, /*index=5*/f32[8,3,128]{2,1,0:T(4...) while((s32[]{:T(128)}, f32[8,3,128]{2,1,0:T(4,128)S(1)}, ...), condition=%wide.region_29.31_spmd.clone, body=%wide.region_25.30_spmd.clone.sunk | while | flops 4610363 | bytes 3891339 | solution.py:100
  361.7 6.8 %all-reduce.4 = (f32[]{:T(128)}, f32[]{:T(128)}) all-reduce(f32[]{:T(128)} %get-tuple-element.560, f32[]{:T(128)} %get-tuple-element.559), channel_id=1, replica_groups=mesh['rep'=2,'gx_0'=4,'gx_1'=16,'gx_2'=2] {'gx_0'}, use_global_device_ids=true, to_apply=%region_19.21 | all-reduce | flops 2 | bytes 16 | tf_op jit(solution)/shard_map/psum | solution.py:65
  368.4 26.8 %all-reduce.1 = (f32[]{:T(128)}, f32[]{:T(128)}) all-reduce(f32[]{:T(128)} %get-tuple-element.619, f32[]{:T(128)} %get-tuple-element.620), channel_id=1, replica_groups=mesh['rep'=2,'gx_0'=4,'gx_1'=16,'gx_2'=2] {'gx_1'}, use_global_device_ids=true, to_apply=%region_20.22 | all-reduce | flops 2 | bytes 16 | tf_op jit(solution)/shard_map/psum | solution.py:65
  395.2 14.1 %all-reduce.7 = (f32[]{:T(128)}, f32[]{:T(128)}) all-reduce(f32[]{:T(128)} %get-tuple-element.613, f32[]{:T(128)} %get-tuple-element.614), channel_id=1, replica_groups=mesh['rep'=2,'gx_0'=4,'gx_1'=16,'gx_2'=2] {'gx_2'}, use_global_device_ids=true, to_apply=%region_21.23 | all-reduce | flops 2 | bytes 16 | tf_op jit(solution)/shard_map/psum | solution.py:65
  437.0 18.2 %all_to_all.66 = f32[64,2,1,1,128]{4,1,3,2,0:T(2,128)S(1)} all-to-all(f32[64,2,1,1,128]{4,1,3,2,0:T(2,128)S(1)} %copy.81), channel_id=1, replica_groups=mesh['rep'=2,'gx_0'=4,'gx_1'=16,'gx_2'=2] {'gx_0','gx_1'}, dimensions={0} | all-to-all | bytes 131072 | tf_op jit(solution)/shard_map/all_to_all | solution.py:53
  473.2 7.8 %all-to-all-done.11 = f32[64,2,1,1,128]{4,1,3,2,0:T(2,128)S(1)} async-done(((f32[64,2,1,1,128]{4,1,3,2,0:T(2,128)}), f32[64,2,1,1,128]{4,1,3,2,0:T(2,128)S(1)}, u32[]{:S(2)}, u32[]{:S(2)}) %all-to-all-start.11) | async-done | bytes 65568 | tf_op jit(solution)/shard_map/all_to_all | solution.py:53
  482.7 43.5 %while.60 = (s32[]{:T(128)}, f32[8,3,128]{2,1,0:T(4,128)S(1)}, s32[8]{0:T(128)S(1)}, s32[8,7]{1,0:T(8,128)}, s32[8]{0:T(128)S(1)}, /*index=5*/f32[8,3,128]{2,1,0...) while((s32[]{:T(128)}, f32[8,3,128]{2,1,0:T(4,128)S(1)}, ...), condition=%wide.region_45.47_spmd.clone, body=%wide.region_41.46_spmd.clone.sunk | while | flops 4610363 | bytes 3891027 | solution.py:100
  544.4 6.7 %all-reduce.3 = (f32[]{:T(128)}, f32[]{:T(128)}) all-reduce(f32[]{:T(128)} %get-tuple-element.558, f32[]{:T(128)} %get-tuple-element.557), channel_id=1, replica_groups=mesh['rep'=2,'gx_0'=4,'gx_1'=16,'gx_2'=2] {'gx_0'}, use_global_device_ids=true, to_apply=%region_35.37 | all-reduce | flops 2 | bytes 16 | tf_op jit(solution)/shard_map/psum | solution.py:65
  551.1 26.5 %all-reduce = (f32[]{:T(128)}, f32[]{:T(128)}) all-reduce(f32[]{:T(128)} %get-tuple-element.617, f32[]{:T(128)} %get-tuple-element.618), channel_id=1, replica_groups=mesh['rep'=2,'gx_0'=4,'gx_1'=16,'gx_2'=2] {'gx_1'}, use_global_device_ids=true, to_apply=%region_36.38 | all-reduce | flops 2 | bytes 16 | tf_op jit(solution)/shard_map/psum | solution.py:65
  577.6 13.9 %all-reduce.6 = (f32[]{:T(128)}, f32[]{:T(128)}) all-reduce(f32[]{:T(128)} %get-tuple-element.611, f32[]{:T(128)} %get-tuple-element.612), channel_id=1, replica_groups=mesh['rep'=2,'gx_0'=4,'gx_1'=16,'gx_2'=2] {'gx_2'}, use_global_device_ids=true, to_apply=%region_37.39 | all-reduce | flops 2 | bytes 16 | tf_op jit(solution)/shard_map/psum | solution.py:65
  (621 shorter events, 293.7 us)
Async XLA Ops:
  15.9 34.8 %collective-permute-start = (f32[1,128,128]{2,1,0:T(8,128)}, f32[1,128,128]{2,1,0:T(8,128)}, u32[]{:S(2)}, u32[]{:S(2)}) collective-permute-start(f32[1,128,128]{2,1,0:T(8,128)} %get-tuple-element.678), channel_id=1, source_target_pairs={{0,127},{1,0},{2,1},{3,2},{4,3},{5,4},{6,5},{7,6},{8,7},{9,8},{10,... | collective-permute-start | bytes 196616 | tf_op jit(solution)/shard_map/ppermute | solution.py:22
  36.4 14.9 %collective-permute-start.1 = (f32[1,128,128]{2,1,0:T(8,128)}, f32[1,128,128]{2,1,0:T(8,128)}, u32[]{:S(2)}, u32[]{:S(2)}) collective-permute-start(f32[1,128,128]{2,1,0:T(8,128)} %get-tuple-element.681), channel_id=1, source_target_pairs={{0,1},{1,2},{2,3},{3,4},{4,5},{5,6},{6,7},{7,8},{8,9},{9,10},{10,1... | collective-permute-start | bytes 196616 | tf_op jit(solution)/shard_map/ppermute | solution.py:22
  36.4 16.1 %collective-permute-start.2 = (f32[1,128,128]{2,1,0:T(8,128)}, f32[1,128,128]{2,1,0:T(8,128)}, u32[]{:S(2)}, u32[]{:S(2)}) collective-permute-start(f32[1,128,128]{2,1,0:T(8,128)} %get-tuple-element.680), channel_id=1, source_target_pairs={{0,126},{1,127},{2,0},{3,1},{4,2},{5,3},{6,4},{7,5},{8,6},{9,7},{1... | collective-permute-start | bytes 196616 | tf_op jit(solution)/shard_map/ppermute | solution.py:22
  46.5 9.7 %collective-permute-start.3 = (f32[1,128,128]{2,1,0:T(8,128)}, f32[1,128,128]{2,1,0:T(8,128)}, u32[]{:S(2)}, u32[]{:S(2)}) collective-permute-start(f32[1,128,128]{2,1,0:T(8,128)} %get-tuple-element.679), channel_id=1, source_target_pairs={{0,2},{1,3},{2,4},{3,5},{4,6},{5,7},{6,8},{7,9},{8,10},{9,11},{10,... | collective-permute-start | bytes 196616 | tf_op jit(solution)/shard_map/ppermute | solution.py:22
  47.1 27.5 %collective-permute-start.8 = (f32[3,384]{1,0:T(4,128)}, f32[3,384]{1,0:T(4,128)}, u32[]{:S(2)}, u32[]{:S(2)}) collective-permute-start(f32[3,384]{1,0:T(4,128)} %get-tuple-element.708), channel_id=1, source_target_pairs={{0,1},{1,2},{2,3},{3,4},{4,5},{5,6},{6,7},{7,8},{8,9},{9,10},{10,1... | collective-permute-start | bytes 13832 | tf_op jit(solution)/shard_map/ppermute | solution.py:32
  50.7 24.7 %collective-permute-start.9 = (f32[3,384]{1,0:T(4,128)}, f32[3,384]{1,0:T(4,128)}, u32[]{:S(2)}, u32[]{:S(2)}) collective-permute-start(f32[3,384]{1,0:T(4,128)} %get-tuple-element.707), channel_id=1, source_target_pairs={{1,0},{2,1},{3,2},{4,3},{5,4},{6,5},{7,6},{8,7},{9,8},{10,9},{11,1... | collective-permute-start | bytes 13832 | tf_op jit(solution)/shard_map/ppermute | solution.py:33
  51.2 51.5 %collective-permute-start.10 = (f32[3,384]{1,0:T(4,128)}, f32[3,384]{1,0:T(4,128)}, u32[]{:S(2)}, u32[]{:S(2)}) collective-permute-start(f32[3,384]{1,0:T(4,128)} %get-tuple-element.705), channel_id=1, source_target_pairs={{0,1},{1,2},{2,3},{3,4},{4,5},{5,6},{6,7},{7,8},{8,9},{9,10},{10,1... | collective-permute-start | bytes 13832 | tf_op jit(solution)/shard_map/ppermute | solution.py:32
  52.5 50.3 %collective-permute-start.11 = (f32[3,384]{1,0:T(4,128)}, f32[3,384]{1,0:T(4,128)}, u32[]{:S(2)}, u32[]{:S(2)}) collective-permute-start(f32[3,384]{1,0:T(4,128)} %get-tuple-element.706), channel_id=1, source_target_pairs={{1,0},{2,1},{3,2},{4,3},{5,4},{6,5},{7,6},{8,7},{9,8},{10,9},{11,1... | collective-permute-start | bytes 13832 | tf_op jit(solution)/shard_map/ppermute | solution.py:33
  68.2 18.6 %all-to-all-start.1 = ((f32[64,2,1,1,128]{4,1,3,2,0:T(2,128)}), f32[64,2,1,1,128]{4,1,3,2,0:T(2,128)S(1)}, u32[]{:S(2)}, u32[]{:S(2)}) async-start(f32[64,2,1,1,128]{4,1,3,2,0:T(2,128)} %copy.69), calls=%async_computation.1 | async-start | bytes 131072 | tf_op jit(solution)/shard_map/all_to_all | solution.py:53
  95.5 18.6 %all-to-all-start.3 = ((f32[64,2,1,1,128]{4,1,3,2,0:T(2,128)}), f32[64,2,1,1,128]{4,1,3,2,0:T(2,128)S(1)}, u32[]{:S(2)}, u32[]{:S(2)}) async-start(f32[64,2,1,1,128]{4,1,3,2,0:T(2,128)} %copy.71), calls=%async_computation.3 | async-start | bytes 131072 | tf_op jit(solution)/shard_map/all_to_all | solution.py:53
  115.3 51.5 %collective-permute-start.4 = (f32[1,128,128]{2,1,0:T(8,128)S(1)}, f32[1,128,128]{2,1,0:T(8,128)S(1)}, u32[]{:S(2)}, u32[]{:S(2)}) collective-permute-start(f32[1,128,128]{2,1,0:T(8,128)S(1)} %convolution_bitcast_fusion.2), channel_id=1, source_target_pairs={{0,2},{1,3},{2,4},{3,5},{4,6},{5,7},{6,8},{7,9},{8,10},{9,11},{10,... | collective-permute-start | bytes 196616 | tf_op jit(solution)/shard_map/ppermute | solution.py:22
  159.4 7.3 %collective-permute-start.5 = (f32[1,128,128]{2,1,0:T(8,128)S(1)}, f32[1,128,128]{2,1,0:T(8,128)S(1)}, u32[]{:S(2)}, u32[]{:S(2)}) collective-permute-start(f32[1,128,128]{2,1,0:T(8,128)S(1)} %convolution_bitcast_fusion.2), channel_id=1, source_target_pairs={{0,1},{1,2},{2,3},{3,4},{4,5},{5,6},{6,7},{7,8},{8,9},{9,10},{10,1... | collective-permute-start | bytes 196616 | tf_op jit(solution)/shard_map/ppermute | solution.py:22
  162.2 6.1 %collective-permute-start.7 = (f32[1,128,128]{2,1,0:T(8,128)S(1)}, f32[1,128,128]{2,1,0:T(8,128)S(1)}, u32[]{:S(2)}, u32[]{:S(2)}) collective-permute-start(f32[1,128,128]{2,1,0:T(8,128)S(1)} %convolution_bitcast_fusion.2), channel_id=1, source_target_pairs={{0,126},{1,127},{2,0},{3,1},{4,2},{5,3},{6,4},{7,5},{8,6},{9,7},{1... | collective-permute-start | bytes 196616 | tf_op jit(solution)/shard_map/ppermute | solution.py:22
  231.7 5.7 collective-permute-start.12
  237.4 6.4 %collective-permute-start.15 = (f32[1,128,128]{2,1,0:T(8,128)S(1)}, f32[1,128,128]{2,1,0:T(8,128)S(1)}, u32[]{:S(2)}, u32[]{:S(2)}) collective-permute-start(f32[1,128,128]{2,1,0:T(8,128)S(1)} %get-tuple-element.675), channel_id=1, source_target_pairs={{0,2},{1,3},{2,4},{3,5},{4,6},{5,7},{6,8},{7,9},{8,10},{9,11},{10,... | collective-permute-start | bytes 196616 | tf_op jit(solution)/shard_map/ppermute | solution.py:22
  273.6 18.6 %all-to-all-start.7 = ((f32[64,2,1,1,128]{4,1,3,2,0:T(2,128)}), f32[64,2,1,1,128]{4,1,3,2,0:T(2,128)S(1)}, u32[]{:S(2)}, u32[]{:S(2)}) async-start(f32[64,2,1,1,128]{4,1,3,2,0:T(2,128)} %copy.77), calls=%async_computation.7 | async-start | bytes 131072 | tf_op jit(solution)/shard_map/all_to_all | solution.py:53
  293.4 57.1 %collective-permute-start.16 = (f32[1,128,128]{2,1,0:T(8,128)S(1)}, f32[1,128,128]{2,1,0:T(8,128)S(1)}, u32[]{:S(2)}, u32[]{:S(2)}) collective-permute-start(f32[1,128,128]{2,1,0:T(8,128)S(1)} %convolution_bitcast_fusion.1), channel_id=1, source_target_pairs={{0,2},{1,3},{2,4},{3,5},{4,6},{5,7},{6,8},{7,9},{8,10},{9,11},{10,... | collective-permute-start | bytes 196616 | tf_op jit(solution)/shard_map/ppermute | solution.py:22
  343.2 7.3 %collective-permute-start.17 = (f32[1,128,128]{2,1,0:T(8,128)S(1)}, f32[1,128,128]{2,1,0:T(8,128)S(1)}, u32[]{:S(2)}, u32[]{:S(2)}) collective-permute-start(f32[1,128,128]{2,1,0:T(8,128)S(1)} %convolution_bitcast_fusion.1), channel_id=1, source_target_pairs={{0,1},{1,2},{2,3},{3,4},{4,5},{5,6},{6,7},{7,8},{8,9},{9,10},{10,1... | collective-permute-start | bytes 196616 | tf_op jit(solution)/shard_map/ppermute | solution.py:22
  346.2 5.6 collective-permute-start.19
  425.8 6.4 %collective-permute-start.25 = (f32[1,128,128]{2,1,0:T(8,128)S(1)}, f32[1,128,128]{2,1,0:T(8,128)S(1)}, u32[]{:S(2)}, u32[]{:S(2)}) collective-permute-start(f32[1,128,128]{2,1,0:T(8,128)S(1)} %get-tuple-element.671), channel_id=1, source_target_pairs={{0,2},{1,3},{2,4},{3,5},{4,6},{5,7},{6,8},{7,9},{8,10},{9,11},{10,... | collective-permute-start | bytes 196616 | tf_op jit(solution)/shard_map/ppermute | solution.py:22
  462.4 18.6 %all-to-all-start.11 = ((f32[64,2,1,1,128]{4,1,3,2,0:T(2,128)}), f32[64,2,1,1,128]{4,1,3,2,0:T(2,128)S(1)}, u32[]{:S(2)}, u32[]{:S(2)}) async-start(f32[64,2,1,1,128]{4,1,3,2,0:T(2,128)} %copy.83), calls=%async_computation.11 | async-start | bytes 131072 | tf_op jit(solution)/shard_map/all_to_all | solution.py:53
  482.1 51.5 %collective-permute-start.26 = (f32[1,128,128]{2,1,0:T(8,128)S(1)}, f32[1,128,128]{2,1,0:T(8,128)S(1)}, u32[]{:S(2)}, u32[]{:S(2)}) collective-permute-start(f32[1,128,128]{2,1,0:T(8,128)S(1)} %convolution_bitcast_fusion), channel_id=1, source_target_pairs={{0,2},{1,3},{2,4},{3,5},{4,6},{5,7},{6,8},{7,9},{8,10},{9,11},{10,... | collective-permute-start | bytes 196616 | tf_op jit(solution)/shard_map/ppermute | solution.py:22
  526.2 7.4 %collective-permute-start.27 = (f32[1,128,128]{2,1,0:T(8,128)S(1)}, f32[1,128,128]{2,1,0:T(8,128)S(1)}, u32[]{:S(2)}, u32[]{:S(2)}) collective-permute-start(f32[1,128,128]{2,1,0:T(8,128)S(1)} %convolution_bitcast_fusion), channel_id=1, source_target_pairs={{0,1},{1,2},{2,3},{3,4},{4,5},{5,6},{6,7},{7,8},{8,9},{9,10},{10,1... | collective-permute-start | bytes 196616 | tf_op jit(solution)/shard_map/ppermute | solution.py:22
  529.0 6.3 %collective-permute-start.29 = (f32[1,128,128]{2,1,0:T(8,128)S(1)}, f32[1,128,128]{2,1,0:T(8,128)S(1)}, u32[]{:S(2)}, u32[]{:S(2)}) collective-permute-start(f32[1,128,128]{2,1,0:T(8,128)S(1)} %convolution_bitcast_fusion), channel_id=1, source_target_pairs={{0,126},{1,127},{2,0},{3,1},{4,2},{5,3},{6,4},{7,5},{8,6},{9,7},{1... | collective-permute-start | bytes 196616 | tf_op jit(solution)/shard_map/ppermute | solution.py:22
  (54 other events, 793.4 us)
where the time goes:
time: 608 us; the launch traced here: 596 us
  blocking collectives  210 us (35%)
  starting transfers between devices  98.1 us (16%)
  other arithmetic  74.3 us (12%)
  local copies, waits for them, and re-layouts  73.3 us (12%)
  waiting for transfers between devices  61.1 us (10%)
  matrix products  50.9 us (8%)
  loops' own time  17.2 us (3%)
  between operations  11.9 us (2%)
    psum x9, blocking collectives, over_axes(): x = lax.psum(x, axis)  142 us
    all_to_all x8, blocking collectives, turned_blocks(): lax.all_to_all(tiles, axes[k], split_axis=k, concat_axis=k, tiled=True)  67.7 us
    ppermute x24, starting transfers between devices, from_behind(): lax.ppermute(x, axis, [(i, (i + by) % devices) for i in range(devices)])  65.1 us
    all_to_all x4, waiting for transfers between devices, turned_blocks(): lax.all_to_all(tiles, axes[k], split_axis=k, concat_axis=k, tiled=True)  37.1 us
    dynamic_slice x48, local copies, waits for them, and re-layouts, pair_field(): lax.scan(one_block, jnp.zeros((), jnp.float32), (home_blocks, tile_rows,...  33.4 us
    and x24, other arithmetic, one_block(): near_pos = jnp.take(pos_blocks, tile_row, axis=1)  31.9 us
    all_to_all x4, starting transfers between devices, turned_blocks(): lax.all_to_all(tiles, axes[k], split_axis=k, concat_axis=k, tiled=True)  25.8 us
    another operation x3, loops' own time, pair_field(): lax.scan(one_block, jnp.zeros((), jnp.float32), (home_blocks, tile_rows,...  17.2 us
  transfers between devices with their start and end apart: 36, of which 15 were waited for; matrix products, arithmetic and copies ran while one was open for 22% of the time, Pallas kernels for 0%

commit v1 on v0

--- a/solution.py
+++ b/solution.py
@@ -62,7 +62,7 @@
 
 def over_axes(x, axes):
     for axis in axes:
-        x = lax.psum(x, axis)
+        x = jnp.sum(lax.all_gather(x, axis), axis=0)
     return x
 
 

time: 608 us -> 641 us (1.054)
  local copies, waits for them, and re-layouts: 73.3 us -> 102 us
  other arithmetic: 74.3 us -> 85.1 us
    psum x9 -> x0, blocking collectives: 142 us -> none  [over_axes(): x = lax.psum(x, axis)]
    unnamed x0 -> x9, blocking collectives: none -> 136 us
    unnamed x66 -> x107, local copies, waits for them, and re-layouts: 1.51 us -> 29.6 us
    reduce_sum x0 -> x18, other arithmetic: none -> 10.9 us  [over_axes(): x = jnp.sum(lax.all_gather(x, axis), axis=0)]
where the time goes in v1:
time: 641 us; the launch traced here: 629 us
  blocking collectives  204 us (32%)
  local copies, waits for them, and re-layouts  102 us (16%)
  starting transfers between devices  98 us (15%)
  other arithmetic  85.1 us (13%)
  waiting for transfers between devices  61 us (10%)
  matrix products  50.7 us (8%)
  loops' own time  16.7 us (3%)
  between operations  11.8 us (2%)
    unnamed x9, blocking collectives  136 us
    all_to_all x8, blocking collectives, turned_blocks(): lax.all_to_all(tiles, axes[k], split_axis=k, concat_axis=k, tiled=True)  67.7 us
    ppermute x24, starting transfers between devices, from_behind(): lax.ppermute(x, axis, [(i, (i + by) % devices) for i in range(devices)])  65 us
    all_to_all x4, waiting for transfers between devices, turned_blocks(): lax.all_to_all(tiles, axes[k], split_axis=k, concat_axis=k, tiled=True)  37.1 us
    dynamic_slice x48, local copies, waits for them, and re-layouts, pair_field(): lax.scan(one_block, jnp.zeros((), jnp.float32), (home_blocks, tile_rows,...  34.2 us
    and x24, other arithmetic, one_block(): near_pos = jnp.take(pos_blocks, tile_row, axis=1)  32 us
    unnamed x107, local copies, waits for them, and re-layouts  29.6 us
    all_to_all x4, starting transfers between devices, turned_blocks(): lax.all_to_all(tiles, axes[k], split_axis=k, concat_axis=k, tiled=True)  25.9 us
  transfers between devices with their start and end apart: 36, of which 15 were waited for; matrix products, arithmetic and copies ran while one was open for 22% of the time, Pallas kernels for 0%

profile of v1, /device:TPU:33, one launch (start us, length us, event | category | flops | bytes accessed | tf_op | source)
XLA Modules:
  0.0 629.1 jit_solution(666603174821779447)
XLA Ops:
  15.9 20.4 %collective-permute-start = (f32[1,128,128]{2,1,0:T(8,128)}, f32[1,128,128]{2,1,0:T(8,128)}, u32[]{:S(2)}, u32[]{:S(2)}) collective-permute-start(f32[1,128,128]{2,1,0:T(8,128)} %get-tuple-element.678), channel_id=1, source_target_pairs={{0,127},{1,0},{2,1},{3,2},{4,3},{5,4},{6,5},{7,6},{8,7},{9,8},{10,... | collective-permute-start | bytes 196616 | tf_op jit(solution)/shard_map/ppermute | solution.py:22
  36.4 10.2 %collective-permute-start.2 = (f32[1,128,128]{2,1,0:T(8,128)}, f32[1,128,128]{2,1,0:T(8,128)}, u32[]{:S(2)}, u32[]{:S(2)}) collective-permute-start(f32[1,128,128]{2,1,0:T(8,128)} %get-tuple-element.680), channel_id=1, source_target_pairs={{0,126},{1,127},{2,0},{3,1},{4,2},{5,3},{6,4},{7,5},{8,6},{9,7},{1... | collective-permute-start | bytes 196616 | tf_op jit(solution)/shard_map/ppermute | solution.py:22
  61.5 8.4 %all_to_all.60 = f32[64,2,1,1,128]{4,0,3,2,1:T(8,128)S(1)} all-to-all(f32[64,2,1,1,128]{4,0,3,2,1:T(8,128)S(1)} %copy.68), channel_id=1, replica_groups=mesh['rep'=2,'gx_0'=4,'gx_1'=16,'gx_2'=2] {'gx_2'}, dimensions={1} | all-to-all | bytes 131072 | tf_op jit(solution)/shard_map/all_to_all | solution.py:53
  70.5 6.5 %all-to-all-start.1 = ((f32[64,2,1,1,128]{4,1,3,2,0:T(2,128)}), f32[64,2,1,1,128]{4,1,3,2,0:T(2,128)S(1)}, u32[]{:S(2)}, u32[]{:S(2)}) async-start(f32[64,2,1,1,128]{4,1,3,2,0:T(2,128)} %copy.69), calls=%async_computation.1 | async-start | bytes 131072 | tf_op jit(solution)/shard_map/all_to_all | solution.py:53
  78.4 10.7 %all-to-all-done.1 = f32[64,2,1,1,128]{4,1,3,2,0:T(2,128)S(1)} async-done(((f32[64,2,1,1,128]{4,1,3,2,0:T(2,128)}), f32[64,2,1,1,128]{4,1,3,2,0:T(2,128)S(1)}, u32[]{:S(2)}, u32[]{:S(2)}) %all-to-all-start.1) | async-done | bytes 65568 | tf_op jit(solution)/shard_map/all_to_all | solution.py:53
  97.7 6.5 %all-to-all-start.3 = ((f32[64,2,1,1,128]{4,1,3,2,0:T(2,128)}), f32[64,2,1,1,128]{4,1,3,2,0:T(2,128)S(1)}, u32[]{:S(2)}, u32[]{:S(2)}) async-start(f32[64,2,1,1,128]{4,1,3,2,0:T(2,128)} %copy.71), calls=%async_computation.3 | async-start | bytes 131072 | tf_op jit(solution)/shard_map/all_to_all | solution.py:53
  105.8 10.6 %all-to-all-done.3 = f32[64,2,1,1,128]{4,1,3,2,0:T(2,128)S(1)} async-done(((f32[64,2,1,1,128]{4,1,3,2,0:T(2,128)}), f32[64,2,1,1,128]{4,1,3,2,0:T(2,128)S(1)}, u32[]{:S(2)}, u32[]{:S(2)}) %all-to-all-start.3) | async-done | bytes 65568 | tf_op jit(solution)/shard_map/all_to_all | solution.py:53
  118.0 43.6 %while.58 = (s32[]{:T(128)}, f32[8,3,128]{2,1,0:T(4,128)S(1)}, s32[8]{0:T(128)S(1)}, s32[8,7]{1,0:T(8,128)}, s32[8]{0:T(128)S(1)}, /*index=5*/f32[8,3,128]{2,1,0...) while((s32[]{:T(128)}, f32[8,3,128]{2,1,0:T(4,128)S(1)}, ...), condition=%wide.region_13.15_spmd.clone, body=%wide.region_9.14_spmd.clone.sunk | while | flops 4610363 | bytes 3891027 | solution.py:100
  192.3 25.9 %all-reduce.20 = (f32[16]{0:T(128)S(1)}, f32[16]{0:T(128)S(1)}) all-reduce(f32[16]{0:T(128)S(1)} %dynamic-update-slice.28, f32[16]{0:T(128)S(1)} %dynamic-update-slice.31), channel_id=1, replica_groups=mesh['rep'=2,'gx_0'=4,'gx_1'=16,'gx_2'=2] {'gx_1'}, use_global_device_ids=true, to_apply=%add.1 | all-reduce | flops 32 | bytes 256
  222.2 13.2 %all-reduce.26 = (f32[2]{0:T(128)S(1)}, f32[2]{0:T(128)S(1)}) all-reduce(f32[2]{0:T(128)S(1)} %dynamic-update-slice.29, f32[2]{0:T(128)S(1)} %dynamic-update-slice.32), channel_id=1, replica_groups=mesh['rep'=2,'gx_0'=4,'gx_1'=16,'gx_2'=2] {'gx_2'}, use_global_device_ids=true, to_apply=%add.2 | all-reduce | flops 4 | bytes 32
  261.3 17.8 %all_to_all.63 = f32[64,2,1,1,128]{4,1,3,2,0:T(2,128)S(1)} all-to-all(f32[64,2,1,1,128]{4,1,3,2,0:T(2,128)S(1)} %copy.75), channel_id=1, replica_groups=mesh['rep'=2,'gx_0'=4,'gx_1'=16,'gx_2'=2] {'gx_0','gx_1'}, dimensions={0} | all-to-all | bytes 131072 | tf_op jit(solution)/shard_map/all_to_all | solution.py:53
  286.4 6.5 %all-to-all-start.7 = ((f32[64,2,1,1,128]{4,1,3,2,0:T(2,128)}), f32[64,2,1,1,128]{4,1,3,2,0:T(2,128)S(1)}, u32[]{:S(2)}, u32[]{:S(2)}) async-start(f32[64,2,1,1,128]{4,1,3,2,0:T(2,128)} %copy.77), calls=%async_computation.7 | async-start | bytes 131072 | tf_op jit(solution)/shard_map/all_to_all | solution.py:53
  297.1 7.9 %all-to-all-done.7 = f32[64,2,1,1,128]{4,1,3,2,0:T(2,128)S(1)} async-done(((f32[64,2,1,1,128]{4,1,3,2,0:T(2,128)}), f32[64,2,1,1,128]{4,1,3,2,0:T(2,128)S(1)}, u32[]{:S(2)}, u32[]{:S(2)}) %all-to-all-start.7) | async-done | bytes 65568 | tf_op jit(solution)/shard_map/all_to_all | solution.py:53
  307.5 48.9 %while.59 = (s32[]{:T(128)}, f32[8,3,128]{2,1,0:T(4,128)S(1)}, s32[8]{0:T(128)S(1)}, s32[8,7]{1,0:T(8,128)}, s32[8]{0:T(128)}, /*index=5*/f32[8,3,128]{2,1,0:T(4...) while((s32[]{:T(128)}, f32[8,3,128]{2,1,0:T(4,128)S(1)}, ...), condition=%wide.region_29.31_spmd.clone, body=%wide.region_25.30_spmd.clone.sunk | while | flops 4610363 | bytes 3891339 | solution.py:100
  377.5 6.1 all-reduce.22
  387.4 26.1 %all-reduce.19 = (f32[16]{0:T(128)S(1)}, f32[16]{0:T(128)S(1)}) all-reduce(f32[16]{0:T(128)S(1)} %dynamic-update-slice.34, f32[16]{0:T(128)S(1)} %dynamic-update-slice.37), channel_id=1, replica_groups=mesh['rep'=2,'gx_0'=4,'gx_1'=16,'gx_2'=2] {'gx_1'}, use_global_device_ids=true, to_apply=%add.7 | all-reduce | flops 32 | bytes 256
  417.5 13.4 %all-reduce.25 = (f32[2]{0:T(128)S(1)}, f32[2]{0:T(128)S(1)}) all-reduce(f32[2]{0:T(128)S(1)} %dynamic-update-slice.35, f32[2]{0:T(128)S(1)} %dynamic-update-slice.38), channel_id=1, replica_groups=mesh['rep'=2,'gx_0'=4,'gx_1'=16,'gx_2'=2] {'gx_2'}, use_global_device_ids=true, to_apply=%add.8 | all-reduce | flops 4 | bytes 32
  459.6 18.4 %all_to_all.66 = f32[64,2,1,1,128]{4,1,3,2,0:T(2,128)S(1)} all-to-all(f32[64,2,1,1,128]{4,1,3,2,0:T(2,128)S(1)} %copy.81), channel_id=1, replica_groups=mesh['rep'=2,'gx_0'=4,'gx_1'=16,'gx_2'=2] {'gx_0','gx_1'}, dimensions={0} | all-to-all | bytes 131072 | tf_op jit(solution)/shard_map/all_to_all | solution.py:53
  485.2 6.5 %all-to-all-start.11 = ((f32[64,2,1,1,128]{4,1,3,2,0:T(2,128)}), f32[64,2,1,1,128]{4,1,3,2,0:T(2,128)S(1)}, u32[]{:S(2)}, u32[]{:S(2)}) async-start(f32[64,2,1,1,128]{4,1,3,2,0:T(2,128)} %copy.83), calls=%async_computation.11 | async-start | bytes 131072 | tf_op jit(solution)/shard_map/all_to_all | solution.py:53
  496.0 7.8 %all-to-all-done.11 = f32[64,2,1,1,128]{4,1,3,2,0:T(2,128)S(1)} async-done(((f32[64,2,1,1,128]{4,1,3,2,0:T(2,128)}), f32[64,2,1,1,128]{4,1,3,2,0:T(2,128)S(1)}, u32[]{:S(2)}, u32[]{:S(2)}) %all-to-all-start.11) | async-done | bytes 65568 | tf_op jit(solution)/shard_map/all_to_all | solution.py:53
  505.5 43.7 %while.60 = (s32[]{:T(128)}, f32[8,3,128]{2,1,0:T(4,128)S(1)}, s32[8]{0:T(128)S(1)}, s32[8,7]{1,0:T(8,128)}, s32[8]{0:T(128)S(1)}, /*index=5*/f32[8,3,128]{2,1,0...) while((s32[]{:T(128)}, f32[8,3,128]{2,1,0:T(4,128)S(1)}, ...), condition=%wide.region_45.47_spmd.clone, body=%wide.region_41.46_spmd.clone.sunk | while | flops 4610363 | bytes 3891027 | solution.py:100
  570.0 6.0 all-reduce.21
  579.9 26.0 %all-reduce.18 = (f32[16]{0:T(128)S(1)}, f32[16]{0:T(128)S(1)}) all-reduce(f32[16]{0:T(128)S(1)} %dynamic-update-slice.40, f32[16]{0:T(128)S(1)} %dynamic-update-slice.43), channel_id=1, replica_groups=mesh['rep'=2,'gx_0'=4,'gx_1'=16,'gx_2'=2] {'gx_1'}, use_global_device_ids=true, to_apply=%add.13 | all-reduce | flops 32 | bytes 256
  609.9 13.2 %all-reduce.24 = (f32[2]{0:T(128)S(1)}, f32[2]{0:T(128)S(1)}) all-reduce(f32[2]{0:T(128)S(1)} %dynamic-update-slice.41, f32[2]{0:T(128)S(1)} %dynamic-update-slice.44), channel_id=1, replica_groups=mesh['rep'=2,'gx_0'=4,'gx_1'=16,'gx_2'=2] {'gx_2'}, use_global_device_ids=true, to_apply=%add.14 | all-reduce | flops 4 | bytes 32
  (680 shorter events, 332.6 us)
Async XLA Ops:
  15.9 37.2 %collective-permute-start = (f32[1,128,128]{2,1,0:T(8,128)}, f32[1,128,128]{2,1,0:T(8,128)}, u32[]{:S(2)}, u32[]{:S(2)}) collective-permute-start(f32[1,128,128]{2,1,0:T(8,128)} %get-tuple-element.678), channel_id=1, source_target_pairs={{0,127},{1,0},{2,1},{3,2},{4,3},{5,4},{6,5},{7,6},{8,7},{9,8},{10,... | collective-permute-start | bytes 196616 | tf_op jit(solution)/shard_map/ppermute | solution.py:22
  36.4 17.3 %collective-permute-start.1 = (f32[1,128,128]{2,1,0:T(8,128)}, f32[1,128,128]{2,1,0:T(8,128)}, u32[]{:S(2)}, u32[]{:S(2)}) collective-permute-start(f32[1,128,128]{2,1,0:T(8,128)} %get-tuple-element.681), channel_id=1, source_target_pairs={{0,1},{1,2},{2,3},{3,4},{4,5},{5,6},{6,7},{7,8},{8,9},{9,10},{10,1... | collective-permute-start | bytes 196616 | tf_op jit(solution)/shard_map/ppermute | solution.py:22
  36.4 18.8 %collective-permute-start.2 = (f32[1,128,128]{2,1,0:T(8,128)}, f32[1,128,128]{2,1,0:T(8,128)}, u32[]{:S(2)}, u32[]{:S(2)}) collective-permute-start(f32[1,128,128]{2,1,0:T(8,128)} %get-tuple-element.680), channel_id=1, source_target_pairs={{0,126},{1,127},{2,0},{3,1},{4,2},{5,3},{6,4},{7,5},{8,6},{9,7},{1... | collective-permute-start | bytes 196616 | tf_op jit(solution)/shard_map/ppermute | solution.py:22
  46.5 12.2 %collective-permute-start.3 = (f32[1,128,128]{2,1,0:T(8,128)}, f32[1,128,128]{2,1,0:T(8,128)}, u32[]{:S(2)}, u32[]{:S(2)}) collective-permute-start(f32[1,128,128]{2,1,0:T(8,128)} %get-tuple-element.679), channel_id=1, source_target_pairs={{0,2},{1,3},{2,4},{3,5},{4,6},{5,7},{6,8},{7,9},{8,10},{9,11},{10,... | collective-permute-start | bytes 196616 | tf_op jit(solution)/shard_map/ppermute | solution.py:22
  47.1 29.9 %collective-permute-start.8 = (f32[3,384]{1,0:T(4,128)}, f32[3,384]{1,0:T(4,128)}, u32[]{:S(2)}, u32[]{:S(2)}) collective-permute-start(f32[3,384]{1,0:T(4,128)} %get-tuple-element.708), channel_id=1, source_target_pairs={{0,1},{1,2},{2,3},{3,4},{4,5},{5,6},{6,7},{7,8},{8,9},{9,10},{10,1... | collective-permute-start | bytes 13832 | tf_op jit(solution)/shard_map/ppermute | solution.py:32
  53.2 24.5 %collective-permute-start.9 = (f32[3,384]{1,0:T(4,128)}, f32[3,384]{1,0:T(4,128)}, u32[]{:S(2)}, u32[]{:S(2)}) collective-permute-start(f32[3,384]{1,0:T(4,128)} %get-tuple-element.707), channel_id=1, source_target_pairs={{1,0},{2,1},{3,2},{4,3},{5,4},{6,5},{7,6},{8,7},{9,8},{10,9},{11,1... | collective-permute-start | bytes 13832 | tf_op jit(solution)/shard_map/ppermute | solution.py:33
  53.7 51.3 %collective-permute-start.10 = (f32[3,384]{1,0:T(4,128)}, f32[3,384]{1,0:T(4,128)}, u32[]{:S(2)}, u32[]{:S(2)}) collective-permute-start(f32[3,384]{1,0:T(4,128)} %get-tuple-element.705), channel_id=1, source_target_pairs={{0,1},{1,2},{2,3},{3,4},{4,5},{5,6},{6,7},{7,8},{8,9},{9,10},{10,1... | collective-permute-start | bytes 13832 | tf_op jit(solution)/shard_map/ppermute | solution.py:32
  55.1 49.9 %collective-permute-start.11 = (f32[3,384]{1,0:T(4,128)}, f32[3,384]{1,0:T(4,128)}, u32[]{:S(2)}, u32[]{:S(2)}) collective-permute-start(f32[3,384]{1,0:T(4,128)} %get-tuple-element.706), channel_id=1, source_target_pairs={{1,0},{2,1},{3,2},{4,3},{5,4},{6,5},{7,6},{8,7},{9,8},{10,9},{11,1... | collective-permute-start | bytes 13832 | tf_op jit(solution)/shard_map/ppermute | solution.py:33
  70.5 18.6 %all-to-all-start.1 = ((f32[64,2,1,1,128]{4,1,3,2,0:T(2,128)}), f32[64,2,1,1,128]{4,1,3,2,0:T(2,128)S(1)}, u32[]{:S(2)}, u32[]{:S(2)}) async-start(f32[64,2,1,1,128]{4,1,3,2,0:T(2,128)} %copy.69), calls=%async_computation.1 | async-start | bytes 131072 | tf_op jit(solution)/shard_map/all_to_all | solution.py:53
  97.7 18.6 %all-to-all-start.3 = ((f32[64,2,1,1,128]{4,1,3,2,0:T(2,128)}), f32[64,2,1,1,128]{4,1,3,2,0:T(2,128)S(1)}, u32[]{:S(2)}, u32[]{:S(2)}) async-start(f32[64,2,1,1,128]{4,1,3,2,0:T(2,128)} %copy.71), calls=%async_computation.3 | async-start | bytes 131072 | tf_op jit(solution)/shard_map/all_to_all | solution.py:53
  117.5 51.5 %collective-permute-start.4 = (f32[1,128,128]{2,1,0:T(8,128)S(1)}, f32[1,128,128]{2,1,0:T(8,128)S(1)}, u32[]{:S(2)}, u32[]{:S(2)}) collective-permute-start(f32[1,128,128]{2,1,0:T(8,128)S(1)} %convolution_bitcast_fusion.2), channel_id=1, source_target_pairs={{0,2},{1,3},{2,4},{3,5},{4,6},{5,7},{6,8},{7,9},{8,10},{9,11},{10,... | collective-permute-start | bytes 196616 | tf_op jit(solution)/shard_map/ppermute | solution.py:22
  161.7 7.3 %collective-permute-start.5 = (f32[1,128,128]{2,1,0:T(8,128)S(1)}, f32[1,128,128]{2,1,0:T(8,128)S(1)}, u32[]{:S(2)}, u32[]{:S(2)}) collective-permute-start(f32[1,128,128]{2,1,0:T(8,128)S(1)} %convolution_bitcast_fusion.2), channel_id=1, source_target_pairs={{0,1},{1,2},{2,3},{3,4},{4,5},{5,6},{6,7},{7,8},{8,9},{9,10},{10,1... | collective-permute-start | bytes 196616 | tf_op jit(solution)/shard_map/ppermute | solution.py:22
  164.5 6.1 collective-permute-start.7
  244.5 5.7 collective-permute-start.12
  250.2 6.4 %collective-permute-start.15 = (f32[1,128,128]{2,1,0:T(8,128)S(1)}, f32[1,128,128]{2,1,0:T(8,128)S(1)}, u32[]{:S(2)}, u32[]{:S(2)}) collective-permute-start(f32[1,128,128]{2,1,0:T(8,128)S(1)} %get-tuple-element.675), channel_id=1, source_target_pairs={{0,2},{1,3},{2,4},{3,5},{4,6},{5,7},{6,8},{7,9},{8,10},{9,11},{10,... | collective-permute-start | bytes 196616 | tf_op jit(solution)/shard_map/ppermute | solution.py:22
  286.4 18.6 %all-to-all-start.7 = ((f32[64,2,1,1,128]{4,1,3,2,0:T(2,128)}), f32[64,2,1,1,128]{4,1,3,2,0:T(2,128)S(1)}, u32[]{:S(2)}, u32[]{:S(2)}) async-start(f32[64,2,1,1,128]{4,1,3,2,0:T(2,128)} %copy.77), calls=%async_computation.7 | async-start | bytes 131072 | tf_op jit(solution)/shard_map/all_to_all | solution.py:53
  306.2 57.3 %collective-permute-start.16 = (f32[1,128,128]{2,1,0:T(8,128)S(1)}, f32[1,128,128]{2,1,0:T(8,128)S(1)}, u32[]{:S(2)}, u32[]{:S(2)}) collective-permute-start(f32[1,128,128]{2,1,0:T(8,128)S(1)} %convolution_bitcast_fusion.1), channel_id=1, source_target_pairs={{0,2},{1,3},{2,4},{3,5},{4,6},{5,7},{6,8},{7,9},{8,10},{9,11},{10,... | collective-permute-start | bytes 196616 | tf_op jit(solution)/shard_map/ppermute | solution.py:22
  356.4 7.1 %collective-permute-start.17 = (f32[1,128,128]{2,1,0:T(8,128)S(1)}, f32[1,128,128]{2,1,0:T(8,128)S(1)}, u32[]{:S(2)}, u32[]{:S(2)}) collective-permute-start(f32[1,128,128]{2,1,0:T(8,128)S(1)} %convolution_bitcast_fusion.1), channel_id=1, source_target_pairs={{0,1},{1,2},{2,3},{3,4},{4,5},{5,6},{6,7},{7,8},{8,9},{9,10},{10,1... | collective-permute-start | bytes 196616 | tf_op jit(solution)/shard_map/ppermute | solution.py:22
  359.2 5.7 collective-permute-start.19
  448.5 6.4 %collective-permute-start.25 = (f32[1,128,128]{2,1,0:T(8,128)S(1)}, f32[1,128,128]{2,1,0:T(8,128)S(1)}, u32[]{:S(2)}, u32[]{:S(2)}) collective-permute-start(f32[1,128,128]{2,1,0:T(8,128)S(1)} %get-tuple-element.671), channel_id=1, source_target_pairs={{0,2},{1,3},{2,4},{3,5},{4,6},{5,7},{6,8},{7,9},{8,10},{9,11},{10,... | collective-permute-start | bytes 196616 | tf_op jit(solution)/shard_map/ppermute | solution.py:22
  485.2 18.6 %all-to-all-start.11 = ((f32[64,2,1,1,128]{4,1,3,2,0:T(2,128)}), f32[64,2,1,1,128]{4,1,3,2,0:T(2,128)S(1)}, u32[]{:S(2)}, u32[]{:S(2)}) async-start(f32[64,2,1,1,128]{4,1,3,2,0:T(2,128)} %copy.83), calls=%async_computation.11 | async-start | bytes 131072 | tf_op jit(solution)/shard_map/all_to_all | solution.py:53
  505.0 51.6 %collective-permute-start.26 = (f32[1,128,128]{2,1,0:T(8,128)S(1)}, f32[1,128,128]{2,1,0:T(8,128)S(1)}, u32[]{:S(2)}, u32[]{:S(2)}) collective-permute-start(f32[1,128,128]{2,1,0:T(8,128)S(1)} %convolution_bitcast_fusion), channel_id=1, source_target_pairs={{0,2},{1,3},{2,4},{3,5},{4,6},{5,7},{6,8},{7,9},{8,10},{9,11},{10,... | collective-permute-start | bytes 196616 | tf_op jit(solution)/shard_map/ppermute | solution.py:22
  549.3 7.3 %collective-permute-start.27 = (f32[1,128,128]{2,1,0:T(8,128)S(1)}, f32[1,128,128]{2,1,0:T(8,128)S(1)}, u32[]{:S(2)}, u32[]{:S(2)}) collective-permute-start(f32[1,128,128]{2,1,0:T(8,128)S(1)} %convolution_bitcast_fusion), channel_id=1, source_target_pairs={{0,1},{1,2},{2,3},{3,4},{4,5},{5,6},{6,7},{7,8},{8,9},{9,10},{10,1... | collective-permute-start | bytes 196616 | tf_op jit(solution)/shard_map/ppermute | solution.py:22
  552.0 6.0 collective-permute-start.29
  (55 other events, 800.6 us)
